TPU v7x, 32 devices: a whole 2x2x4 slice. The times are simulated.
32 devices in a mesh: expert: 2 (over core), task: 4 (over y, x), shard: 4 (over z).
Axes of the slice: x: 2, y: 2, z: 4, core: 2. Of those that a mesh axis runs over, the one named last changes fastest.
Arguments:
- weights: bfloat16 [4, 2, 8192, 2048], P('task', None, ('expert', 'shard')), may hold values from -6 to 6
- fisher: bfloat16 [4, 2, 8192, 2048], P('task', None, ('expert', 'shard')), may hold values from 0.049804688 to 5
- base_weights: bfloat16 [2, 8192, 2048], P('expert', 'task', 'shard'), may hold values from -6 to 6
- tile_list: int32 [4, 2, 8, 4], P('task'), may hold values from 0 to 7, as said below
- tile_count: int32 [4, 2, 8], P('task'), may hold values from 0 to 4, as said below
Outputs:
- merged: bfloat16 [2, 8192, 2048], P('expert', 'task', 'shard')
Inputs may be any that keep to these rules, and one draw needn't show every extreme that they name: `tile_list`: for each fine-fit, expert and row block the first tile_count entries are distinct tiles of the block, numbered 0 to 7, in ascending order; the remaining entries are 0. `tile_count`: 4 is reached, and for each fine-fit some expert has 4 in every row block.
All inputs are finite; a program needn't handle non-finite values.
Results may differ from a plain program's by a relative error of at most 0.006.
Values may be sent and summed in bfloat16 or wider, within the bound.
A program may use at most 128 MiB of HBM per device.

v0:
```python
import functools

import jax
import jax.numpy as jnp
from jax import lax
from jax.experimental import pallas as pl
from jax.experimental.pallas import tpu as pltpu
from jax.sharding import PartitionSpec as P

TILE = 128
PRIOR_WEIGHT = 0.5
DIRECT = 32
MESH = pl.DeviceIdType.MESH


def pack_body(ids, live, weights, fisher, packed):
    expert, slot = pl.program_id(0), pl.program_id(1)
    kept = live[expert * pl.num_programs(1) + slot].astype(jnp.float32)
    pieces, width = packed.shape[1], packed.shape[-1]
    for piece in range(pieces):
        lanes = pl.ds(piece * width, width)
        share = fisher[0, :, lanes].astype(jnp.float32) * kept
        term = share * weights[0, :, lanes].astype(jnp.float32)
        packed[0, piece, 0, 0] = term.astype(jnp.bfloat16)
        packed[0, piece, 1, 0] = share.astype(jnp.bfloat16)


def pack(ids, live, weights, fisher, pieces):
    experts, rows, columns = weights.shape
    cap = ids.shape[0] // experts
    width = columns // pieces
    tile = pl.BlockSpec(
        (1, TILE, columns), lambda e, k, ids, live: (e, ids[e * cap + k], 0)
    )
    return pl.pallas_call(
        pack_body,
        out_shape=jax.ShapeDtypeStruct(
            (experts, pieces, 2, cap, TILE, width), jnp.bfloat16
        ),
        grid_spec=pltpu.PrefetchScalarGridSpec(
            num_scalar_prefetch=2,
            grid=(experts, cap),
            in_specs=[tile, tile],
            out_specs=pl.BlockSpec(
                (1, pieces, 2, 1, TILE, width), lambda e, k, ids, live: (e, 0, 0, k, 0, 0)
            ),
        ),
        name="pack",
    )(ids, live, weights, fisher)


def exchange_body(sizes, packed, received, send_sem, recv_sem, own_sem):
    experts, tasks, shards = sizes
    blocks = experts * shards
    group = blocks // tasks
    expert, task, shard = (lax.axis_index(a) for a in ("expert", "task", "shard"))
    block = expert * shards + shard
    owner = block // group
    place = block % group
    is_own = owner == task
    order = [(de, ds) for ds in range(shards - 1, -1, -1) for de in range(experts)]

    def outgoing(de, ds):
        to_expert = lax.rem(expert + de, experts)
        to_shard = lax.rem(shard + ds, shards)
        return pltpu.make_async_remote_copy(
            src_ref=packed.at[to_expert, to_shard],
            dst_ref=received.at[task, place],
            send_sem=send_sem.at[de, ds],
            recv_sem=recv_sem.at[task, place],
            device_id=(to_expert, owner, to_shard),
            device_id_type=MESH,
        )

    own = pltpu.make_async_copy(
        packed.at[expert, shard], received.at[task, place], own_sem
    )
    for de, ds in order:
        if (de, ds) == (0, 0):
            pl.when(is_own)(own.start)
            pl.when(jnp.logical_not(is_own))(outgoing(de, ds).start)
        else:
            outgoing(de, ds).start()
    for from_task in range(tasks):
        for at in range(group):
            local = jnp.logical_and(is_own, jnp.logical_and(task == from_task, place == at))
            arriving = pltpu.make_async_remote_copy(
                src_ref=packed.at[0, 0],
                dst_ref=received.at[from_task, at],
                send_sem=send_sem.at[0, 0],
                recv_sem=recv_sem.at[from_task, at],
                device_id=(lax.rem(expert + 1, experts), task, shard),
                device_id_type=MESH,
            )
            pl.when(jnp.logical_not(local))(arriving.wait_recv)
    for de, ds in order:
        if (de, ds) == (0, 0):
            pl.when(is_own)(own.wait)
            pl.when(jnp.logical_not(is_own))(outgoing(de, ds).wait_send)
        else:
            outgoing(de, ds).wait_send()


def exchange(packed, sizes):
    experts, tasks, shards = sizes
    group = experts * shards // tasks
    return pl.pallas_call(
        functools.partial(exchange_body, sizes),
        out_shape=jax.ShapeDtypeStruct((tasks, group) + packed.shape[2:], packed.dtype),
        in_specs=[pl.BlockSpec(memory_space=pl.ANY)],
        out_specs=pl.BlockSpec(memory_space=pl.ANY),
        scratch_shapes=[
            pltpu.SemaphoreType.DMA((experts, shards)),
            pltpu.SemaphoreType.DMA((tasks, group)),
            pltpu.SemaphoreType.DMA,
        ],
        compiler_params=pltpu.CompilerParams(has_side_effects=True),
        name="exchange",
    )(packed)


def merge_body(tasks, slots, live, *refs):
    parts, base, merged = refs[:tasks], refs[tasks], refs[tasks + 1]
    at = pl.program_id(0) * pl.num_programs(1) + pl.program_id(1)
    count = pl.num_programs(0) * pl.num_programs(1)
    numerator = PRIOR_WEIGHT * base[...].astype(jnp.float32)
    denominator = jnp.full(base.shape, PRIOR_WEIGHT, jnp.float32)
    for task, part in enumerate(parts):
        kept = live[task * count + at].astype(jnp.float32)
        numerator += part[0, 0, 0, 0].astype(jnp.float32) * kept
        denominator += part[0, 0, 1, 0].astype(jnp.float32) * kept
    merged[...] = (numerator / denominator).astype(jnp.bfloat16)


def merge(slots, live, received, base):
    tasks, group, _, _, _, width = received.shape
    per_block = slots.shape[0] // (tasks * group)

    def part(task):
        return pl.BlockSpec(
            (1, 1, 2, 1, TILE, width),
            lambda g, j, slots, live: (
                task, g, 0, slots[(task * group + g) * per_block + j], 0, 0
            ),
        )

    rows = pl.BlockSpec((TILE, width), lambda g, j, slots, live: (g * per_block + j, 0))
    return pl.pallas_call(
        functools.partial(merge_body, tasks),
        out_shape=jax.ShapeDtypeStruct(base.shape, jnp.bfloat16),
        grid_spec=pltpu.PrefetchScalarGridSpec(
            num_scalar_prefetch=2,
            grid=(group, per_block),
            in_specs=[part(task) for task in range(tasks)] + [rows],
            out_specs=rows,
        ),
        name="merge",
    )(slots, live, *([received] * tasks), base)


def arrive(like, target, send_sem, recv_sem, peer):
    return pltpu.make_async_remote_copy(
        src_ref=like, dst_ref=target, send_sem=send_sem, recv_sem=recv_sem,
        device_id=peer, device_id_type=MESH,
    )


def spread_body(packed, plan, direct, gathered, plans, p_send, p_recv, d_send, d_recv, g_send, g_recv, own_sem):
    expert, task, shard = (lax.axis_index(a) for a in ("expert", "task", "shard"))
    block = expert * 4 + shard
    owner, place = block // 2, block % 2
    half, x, y = shard // 2, task % 2, task // 2
    peer = (1 - expert, task, shard)
    part = (DIRECT, (TILE - DIRECT) // 2)
    far = pl.ds(pl.multiple_of(2 * (1 - half), 2), 2)

    def straight(de, ds):
        to_expert, to_shard = (expert + de) % 2, (shard + ds) % 4
        rows = packed.at[to_expert, to_shard, :, :, pl.ds(0, DIRECT)]
        return rows, pltpu.make_async_remote_copy(
            src_ref=rows, dst_ref=direct.at[task, place],
            send_sem=d_send.at[de, ds], recv_sem=d_recv.at[task, place],
            device_id=(to_expert, owner, to_shard), device_id_type=MESH,
        )

    def partial(de, dx):
        to_expert, to_x = (expert + de) % 2, (x + dx) % 2
        start = pl.multiple_of(part[0] + part[1] * to_x, 16)
        rows = packed.at[to_expert, far, :, :, pl.ds(start, part[1])]
        return rows, pltpu.make_async_remote_copy(
            src_ref=rows, dst_ref=gathered.at[task],
            send_sem=g_send.at[de, dx], recv_sem=g_recv.at[task],
            device_id=(to_expert, 2 * expert + to_x, shard), device_id_type=MESH,
        )

    def tell(step):
        return pltpu.make_async_remote_copy(
            src_ref=plan, dst_ref=plans.at[task],
            send_sem=p_send.at[step], recv_sem=p_recv.at[task],
            device_id=(expert, (task + step) % 4, shard), device_id_type=MESH,
        )

    told = pltpu.make_async_copy(plan, plans.at[task], own_sem.at[2])
    told.start()
    for step in range(1, 4):
        tell(step).start()
    copies = []
    for de in range(2):
        for dx in (1, 0):
            own = y == expert if (de, dx) == (0, 0) else None
            copies.append((partial(de, dx), own, gathered.at[task], own_sem.at[0]))
    for ds in (2, 1, 3, 0):
        for de in range(2):
            own = owner == task if (de, ds) == (0, 0) else None
            copies.append((straight(de, ds), own, direct.at[task, place], own_sem.at[1]))
    for (rows, copy), own, target, sem in copies:
        if own is None:
            copy.start()
        else:
            pl.when(own)(pltpu.make_async_copy(rows, target, sem).start)
            pl.when(jnp.logical_not(own))(copy.start)
    for source in range(4):
        come = arrive(plans.at[source], plans.at[source], p_send.at[0], p_recv.at[source], peer)
        pl.when(task != source)(come.wait_recv)
        local = jnp.logical_and(y == expert, task == source)
        come = arrive(gathered.at[source], gathered.at[source], g_send.at[0, 0], g_recv.at[source], peer)
        pl.when(jnp.logical_not(local))(come.wait_recv)
        for at in range(2):
            local = jnp.logical_and(owner == task, jnp.logical_and(task == source, place == at))
            come = arrive(direct.at[source, at], direct.at[source, at], d_send.at[0, 0], d_recv.at[source, at], peer)
            pl.when(jnp.logical_not(local))(come.wait_recv)
    told.wait()
    for step in range(1, 4):
        tell(step).wait_send()
    for (rows, copy), own, target, sem in copies:
        if own is None:
            copy.wait_send()
        else:
            pl.when(own)(pltpu.make_async_copy(rows, target, sem).wait)
            pl.when(jnp.logical_not(own))(copy.wait_send)


def spread(packed, plan):
    _, _, _, cap, _, width = packed.shape
    return pl.pallas_call(
        spread_body,
        out_shape=(
            jax.ShapeDtypeStruct((4, 2, 2, cap, DIRECT, width), packed.dtype),
            jax.ShapeDtypeStruct((4, 2, 2, cap, (TILE - DIRECT) // 2, width), packed.dtype),
            jax.ShapeDtypeStruct((4,) + plan.shape, plan.dtype),
        ),
        in_specs=[pl.BlockSpec(memory_space=pl.ANY)] * 2,
        out_specs=(pl.BlockSpec(memory_space=pl.ANY),) * 3,
        scratch_shapes=[
            pltpu.SemaphoreType.DMA((4,)),
            pltpu.SemaphoreType.DMA((4,)),
            pltpu.SemaphoreType.DMA((2, 4)),
            pltpu.SemaphoreType.DMA((4, 2)),
            pltpu.SemaphoreType.DMA((2, 2)),
            pltpu.SemaphoreType.DMA((4,)),
            pltpu.SemaphoreType.DMA((3,)),
        ],
        compiler_params=pltpu.CompilerParams(has_side_effects=True),
        name="spread",
    )(packed, plan)


def deliver_body(packed, sums, near, far, n_send, n_recv, f_send, f_recv, own_sem):
    expert, task, shard = (lax.axis_index(a) for a in ("expert", "task", "shard"))
    block = expert * 4 + shard
    owner, place = block // 2, block % 2
    half, x, y = shard // 2, task % 2, task // 2
    peer = (1 - expert, task, shard)
    rest = pl.ds(DIRECT, TILE - DIRECT)
    is_near = x == half

    def reduced(i):
        return pltpu.make_async_remote_copy(
            src_ref=sums.at[i], dst_ref=far.at[shard % 2, x],
            send_sem=f_send.at[i], recv_sem=f_recv.at[shard % 2, x],
            device_id=(expert, 2 * y + half, 2 * (1 - half) + i), device_id_type=MESH,
        )

    def straight(de, di):
        to_expert = (expert + de) % 2
        to_shard = 2 * half + (shard + di) % 2
        rows = packed.at[to_expert, to_shard, :, :, rest]
        return rows, pltpu.make_async_remote_copy(
            src_ref=rows, dst_ref=near.at[task, place],
            send_sem=n_send.at[de, di], recv_sem=n_recv.at[task, place],
            device_id=(to_expert, owner, to_shard), device_id_type=MESH,
        )

    for i in range(2):
        reduced(i).start()
    own = owner == task
    for de, di in ((0, 1), (1, 1), (1, 0)):
        straight(de, di)[1].start()
    rows, copy = straight(0, 0)
    kept = pltpu.make_async_copy(rows, near.at[task, place], own_sem)
    pl.when(own)(kept.start)
    pl.when(jnp.logical_not(own))(copy.start)

    for at in range(2):
        for source in range(2):
            come = arrive(far.at[at, source], far.at[at, source], f_send.at[0], f_recv.at[at, source], peer)
            pl.when(jnp.logical_not(is_near))(come.wait_recv)
        for source in range(4):
            local = jnp.logical_and(own, jnp.logical_and(task == source, place == at))
            come = arrive(near.at[source, at], near.at[source, at], n_send.at[0, 0], n_recv.at[source, at], peer)
            pl.when(jnp.logical_and(is_near, jnp.logical_not(local)))(come.wait_recv)
    for i in range(2):
        reduced(i).wait_send()
    for de, di in ((0, 1), (1, 1), (1, 0)):
        straight(de, di)[1].wait_send()
    pl.when(own)(kept.wait)
    pl.when(jnp.logical_not(own))(copy.wait_send)


def deliver(packed, sums):
    _, _, _, cap, _, width = packed.shape
    return pl.pallas_call(
        deliver_body,
        out_shape=(
            jax.ShapeDtypeStruct((4, 2, 2, cap, TILE - DIRECT, width), packed.dtype),
            jax.ShapeDtypeStruct((2, 2) + sums.shape[1:], packed.dtype),
        ),
        in_specs=[pl.BlockSpec(memory_space=pl.ANY)] * 2,
        out_specs=(pl.BlockSpec(memory_space=pl.ANY),) * 2,
        scratch_shapes=[
            pltpu.SemaphoreType.DMA((2, 2)),
            pltpu.SemaphoreType.DMA((4, 2)),
            pltpu.SemaphoreType.DMA((2,)),
            pltpu.SemaphoreType.DMA((2, 2)),
            pltpu.SemaphoreType.DMA,
        ],
        compiler_params=pltpu.CompilerParams(has_side_effects=True),
        name="deliver",
    )(packed, sums)


def reduce_body(slots, live, *refs):
    parts, sums = refs[:4], refs[4]
    tile = pl.program_id(0)
    total = jnp.zeros(sums.shape[:2] + sums.shape[3:], jnp.float32)
    for task, part in enumerate(parts):
        kept = live[task * pl.num_programs(0) + tile].astype(jnp.float32)
        total += part[0, :, :, 0].astype(jnp.float32) * kept
    sums[:, :, 0] = total.astype(jnp.bfloat16)


def reduce(slots, live, gathered):
    rows, width = gathered.shape[-2:]
    per_block = slots.shape[0] // 4

    def part(task):
        return pl.BlockSpec(
            (1, 2, 2, 1, rows, width),
            lambda j, slots, live: (task, 0, 0, slots[task * per_block + j], 0, 0),
        )

    return pl.pallas_call(
        reduce_body,
        out_shape=jax.ShapeDtypeStruct((2, 2, per_block, rows, width), jnp.bfloat16),
        grid_spec=pltpu.PrefetchScalarGridSpec(
            num_scalar_prefetch=2,
            grid=(per_block,),
            in_specs=[part(task) for task in range(4)],
            out_specs=pl.BlockSpec((2, 2, 1, rows, width), lambda j, slots, live: (0, 0, j, 0, 0)),
        ),
        name="reduce",
    )(slots, live, *([gathered] * 4))


def finish_body(slots, live, near_flag, *refs):
    direct, near, far, base, merged = refs[:4], refs[4:8], refs[8], refs[9], refs[10]
    at = pl.program_id(0) * pl.num_programs(1) + pl.program_id(1)
    count = pl.num_programs(0) * pl.num_programs(1)
    kept = [live[task * count + at].astype(jnp.float32) for task in range(4)]

    def settle(rows, numerator, denominator):
        numerator += PRIOR_WEIGHT * base[rows].astype(jnp.float32)
        merged[rows] = (numerator / (denominator + PRIOR_WEIGHT)).astype(jnp.bfloat16)

    def added(parts, which):
        return sum(p[0, 0, which, 0].astype(jnp.float32) * k for p, k in zip(parts, kept))

    settle(pl.ds(0, DIRECT), added(direct, 0), added(direct, 1))

    @pl.when(near_flag[0] == 1)
    def _():
        settle(pl.ds(DIRECT, TILE - DIRECT), added(near, 0), added(near, 1))

    @pl.when(near_flag[0] == 0)
    def _():
        size = (TILE - DIRECT) // 2
        for x in range(2):
            settle(
                pl.ds(DIRECT + size * x, size),
                far[0, x, 0, 0].astype(jnp.float32),
                far[0, x, 1, 0].astype(jnp.float32),
            )


def finish(slots, live, near_flag, direct, near, far, base):
    width = base.shape[-1]
    per_block = slots.shape[0] // 8

    def direct_part(task):
        return pl.BlockSpec(
            (1, 1, 2, 1, DIRECT, width),
            lambda g, j, slots, live, flag: (task, g, 0, slots[(task * 2 + g) * per_block + j], 0, 0),
        )

    def near_part(task):
        return pl.BlockSpec(
            (1, 1, 2, 1, TILE - DIRECT, width),
            lambda g, j, slots, live, flag: (
                task, g * flag[0], 0, slots[(task * 2 + g) * per_block + j] * flag[0], 0, 0
            ),
        )

    far_part = pl.BlockSpec(
        (1, 2, 2, 1, (TILE - DIRECT) // 2, width),
        lambda g, j, slots, live, flag: (g * (1 - flag[0]), 0, 0, j * (1 - flag[0]), 0, 0),
    )
    rows = pl.BlockSpec((TILE, width), lambda g, j, slots, live, flag: (g * per_block + j, 0))
    return pl.pallas_call(
        finish_body,
        out_shape=jax.ShapeDtypeStruct(base.shape, jnp.bfloat16),
        grid_spec=pltpu.PrefetchScalarGridSpec(
            num_scalar_prefetch=3,
            grid=(2, per_block),
            in_specs=[direct_part(t) for t in range(4)] + [near_part(t) for t in range(4)] + [far_part, rows],
            out_specs=rows,
        ),
        name="finish",
    )(slots, live, near_flag, *([direct] * 4), *([near] * 4), far, base)


def local(weights, fisher, base_weights, tile_list, tile_count):
    experts, tasks, shards = (lax.axis_size(a) for a in ("expert", "task", "shard"))
    expert, task, shard = (lax.axis_index(a) for a in ("expert", "task", "shard"))
    per_block = weights.shape[2] // TILE
    cap = tile_list.shape[-1]
    group = experts * shards // tasks
    block = expert * shards + shard
    slot_number = jnp.arange(cap, dtype=jnp.int32)

    own_list = lax.dynamic_index_in_dim(tile_list[0], block, 1, keepdims=False)
    own_count = lax.dynamic_index_in_dim(tile_count[0], block, 1, keepdims=False)
    own_live = (slot_number[None, :] < own_count[:, None]).astype(jnp.int32)
    packed = pack(own_list.reshape(-1), own_live.reshape(-1), weights[0], fisher[0], shards)

    marked = jnp.where(slot_number < tile_count[..., None], tile_list, per_block)
    mine = lax.dynamic_index_in_dim(marked[0], expert, 0, keepdims=False)
    small = (experts, tasks, shards) == (2, 4, 4)
    if small:
        plan = jnp.pad(mine, ((0, 0), (0, 128 - cap)))
        direct, gathered, plans = spread(packed, plan)
        plans = plans[:, :, :cap]
    else:
        plans = lax.all_gather(marked[0], "task")
        plans = lax.dynamic_index_in_dim(plans, expert, 1, keepdims=False)

    def lookup(start, count):
        part = lax.dynamic_slice_in_dim(plans, start, count, 1)
        hits = part[..., None] == jnp.arange(per_block, dtype=jnp.int32)
        slots = jnp.sum(hits * slot_number[:, None], axis=2).astype(jnp.int32)
        return slots.reshape(-1), jnp.any(hits, axis=2).astype(jnp.int32).reshape(-1)

    slots, live = lookup(task * group, group)
    if small:
        sums = reduce(*lookup((task // 2) * shards + shard, 1), gathered)
        near, far = deliver(packed, sums)
        flag = (task % 2 == shard // 2).astype(jnp.int32).reshape(1)
        return finish(slots, live, flag, direct, near, far, base_weights[0])[None]
    received = exchange(packed, (experts, tasks, shards))
    return merge(slots, live, received, base_weights[0])[None]


def solution(mesh):
    in_specs = (
        P("task", None, ("expert", "shard"), None),
        P("task", None, ("expert", "shard"), None),
        P("expert", "task", "shard"),
        P("task", None, None, None),
        P("task", None, None),
    )
    out_specs = P("expert", "task", "shard")
    return jax.shard_map(local, mesh=mesh, in_specs=in_specs, out_specs=out_specs, check_vma=False)
```

profile of v0, /device:TPU:1, one launch (start us, length us, event | category | flops | bytes accessed | tf_op | source)
XLA Modules:
  0.0 182.9 jit_solution(935059374586408717)
XLA Ops:
  0.0 0.0 copy-start
  0.0 0.9 dynamic-slice_reduce_fusion
  0.9 0.6 reshape.72.ids
  1.5 0.0 copy-done
  1.5 0.2 fusion.3
  1.7 0.1 compare_convert_fusion
  1.8 0.6 reshape.77.live
  2.3 0.0 copy-start.1
  2.3 10.1 %pack.1.packed = bf16[2,4,2,4,128,512]{5,4,3,2,1,0:T(8,128)(2,1)} custom-call(s32[8]{0:T(128)} %reshape.72.ids, s32[8]{0:T(128)} %reshape.77.live, bf16[2,1024,2048]{2,1,0:T(8,128)(2,1)} %bitcast.11, bf16[2,1024,2048]{2,1,0:T(8,128)(2,1)} %bitcast.12), custom_call_target="tpu_custom_call" | custom-call | tf_op jit(solution)/shard_map/pack/pallas_call | solution.py:35
  12.5 0.0 copy-done.1
  12.5 0.1 copy.8
  12.6 0.6 pad.4.plan
  13.2 67.2 %spread.1 = (bf16[4,2,2,4,32,512]{5,4,3,2,1,0:T(8,128)(2,1)}, bf16[4,2,2,4,48,512]{5,4,3,2,1,0:T(8,128)(2,1)}, s32[4,8,128]{2,1,0:T(8,128)}) custom-call(bf16[2,4,2,4,128,512]{5,4,3,2,1,0:T(8,128)(2,1)} %pack.1.packed, s32[8,128]{1,0:T(8,128)} %pad.4.plan), custom_call_target="tpu_custom_call" | custom-call | tf_op jit(solution)/shard_map/spread/pallas_call | solution.py:245
  80.4 0.7 constant_dynamic-slice_fusion.2
  81.2 0.1 select_reduce_fusion
  81.3 0.6 reshape.73.slots
  81.9 0.1 fusion
  82.0 0.6 reshape.78.live
  82.5 0.7 constant_dynamic-slice_fusion
  83.3 0.1 select_reduce_fusion.1
  83.4 0.6 reshape.76.slots
  84.0 0.1 fusion.1
  84.1 0.7 reshape.81.live
  84.7 7.4 %reduce.7.sums = bf16[2,2,8,48,512]{4,3,2,1,0:T(8,128)(2,1)} custom-call(s32[32]{0:T(128)} %reshape.76.slots, s32[32]{0:T(128)} %reshape.81.live, bf16[4,2,2,4,48,512]{5,4,3,2,1,0:T(8,128)(2,1)} %get-tuple-element.12.refs_0_.refs_1_.refs_2_.refs_3_, bf16[4,2,2,4,48,512]{5,4,3,2,1,0:T(8,128)(2,1)} %get-tuple-element.12.refs_0_.refs_1_.refs_2_.refs_3_, ...), custom_call_target="tpu_custom_call" | custom-call | tf_op jit(solution)/shard_map/reduce/pallas_call | solution.py:362
  92.1 76.0 %deliver.1 = (bf16[4,2,2,4,96,512]{5,4,3,2,1,0:T(8,128)(2,1)}, bf16[2,2,2,8,48,512]{5,4,3,2,1,0:T(8,128)(2,1)}) custom-call(bf16[2,4,2,4,128,512]{5,4,3,2,1,0:T(8,128)(2,1)} %pack.1.packed, bf16[2,2,8,48,512]{4,3,2,1,0:T(8,128)(2,1)} %reduce.7.sums), custom_call_target="tpu_custom_call" | custom-call | tf_op jit(solution)/shard_map/deliver/pallas_call | solution.py:322
  168.1 14.8 %finish.1 = bf16[2048,512]{1,0:T(8,128)(2,1)} custom-call(s32[64]{0:T(128)} %reshape.73.slots, s32[64]{0:T(128)} %reshape.78.live, s32[1]{0:T(128)} %bitcast.4.near_flag, bf16[4,2,2,4,32,512]{5,4,3,2,1,0:T(8,128)(2,1)} %get-tuple-element.11.refs_0_.refs_1_.refs_2_.refs_3_, bf16[4,2,2,4,32,512]{5,4,3,2,1,0:T(8,128)(2,1)} %get-tuple-element.11.refs_0_.refs_1_.refs_2_.refs_3_, ...), custom_call_target="tpu_custom_call" | custom-call | tf_op jit(solution)/shard_map/finish/pallas_call | solution.py:428
  (4 shorter events, 0.0 us)
Async XLA Ops:
  0.0 1.5 copy-start
  2.3 10.1 %copy-start.1 = (s32[1,2,8,4]{2,3,1,0:T(4,128)S(1)}, s32[1,2,8,4]{2,3,1,0:T(4,128)}, u32[]{:S(2)}) copy-start(s32[1,2,8,4]{2,3,1,0:T(4,128)} %param.8) | copy-start | bytes 772
where the time goes:
time: 184 us; the launch traced here: 183 us
  Pallas kernels  176 us (96%)
  local copies, waits for them, and re-layouts  6.87 us (4%)
    pallas_call x1, Pallas kernels, deliver(): pl.pallas_call(deliver_body, out_shape=(jax.ShapeDtypeStruct((4, 2, 2, ca...  76 us
    pallas_call x1, Pallas kernels, spread(): pl.pallas_call(spread_body, out_shape=(jax.ShapeDtypeStruct((4, 2, 2, cap...  67.2 us
    pallas_call x1, Pallas kernels, finish(): pl.pallas_call(finish_body, out_shape=jax.ShapeDtypeStruct(base.shape, jn...  14.8 us
    pallas_call x1, Pallas kernels, pack(): pl.pallas_call(pack_body, out_shape=jax.ShapeDtypeStruct((experts, pieces...  10.1 us
    pallas_call x1, Pallas kernels, reduce(): pl.pallas_call(reduce_body, out_shape=jax.ShapeDtypeStruct((2, 2, per_blo...  7.4 us

commit v1 on v0

v1 whole, which is shorter than its diff:
```python
import functools

import jax
import jax.numpy as jnp
from jax import lax
from jax.experimental import pallas as pl
from jax.experimental.pallas import tpu as pltpu
from jax.sharding import PartitionSpec as P

TILE = 128
PRIOR_WEIGHT = 0.5
DIRECT = 32
MESH = pl.DeviceIdType.MESH


def pack_body(ids, live, weights, fisher, packed):
    expert, slot = pl.program_id(0), pl.program_id(1)
    kept = live[expert * pl.num_programs(1) + slot].astype(jnp.float32)
    pieces, width = packed.shape[1], packed.shape[-1]
    for piece in range(pieces):
        lanes = pl.ds(piece * width, width)
        share = fisher[0, :, lanes].astype(jnp.float32) * kept
        term = share * weights[0, :, lanes].astype(jnp.float32)
        packed[0, piece, 0, 0] = term.astype(jnp.bfloat16)
        packed[0, piece, 1, 0] = share.astype(jnp.bfloat16)


def pack(ids, live, weights, fisher, pieces):
    experts, rows, columns = weights.shape
    cap = ids.shape[0] // experts
    width = columns // pieces
    tile = pl.BlockSpec(
        (1, TILE, columns), lambda e, k, ids, live: (e, ids[e * cap + k], 0)
    )
    return pl.pallas_call(
        pack_body,
        out_shape=jax.ShapeDtypeStruct(
            (experts, pieces, 2, cap, TILE, width), jnp.bfloat16
        ),
        grid_spec=pltpu.PrefetchScalarGridSpec(
            num_scalar_prefetch=2,
            grid=(experts, cap),
            in_specs=[tile, tile],
            out_specs=pl.BlockSpec(
                (1, pieces, 2, 1, TILE, width), lambda e, k, ids, live: (e, 0, 0, k, 0, 0)
            ),
        ),
        name="pack",
    )(ids, live, weights, fisher)


def exchange_body(sizes, packed, received, send_sem, recv_sem, own_sem):
    experts, tasks, shards = sizes
    blocks = experts * shards
    group = blocks // tasks
    expert, task, shard = (lax.axis_index(a) for a in ("expert", "task", "shard"))
    block = expert * shards + shard
    owner = block // group
    place = block % group
    is_own = owner == task
    order = [(de, ds) for ds in range(shards - 1, -1, -1) for de in range(experts)]

    def outgoing(de, ds):
        to_expert = lax.rem(expert + de, experts)
        to_shard = lax.rem(shard + ds, shards)
        return pltpu.make_async_remote_copy(
            src_ref=packed.at[to_expert, to_shard],
            dst_ref=received.at[task, place],
            send_sem=send_sem.at[de, ds],
            recv_sem=recv_sem.at[task, place],
            device_id=(to_expert, owner, to_shard),
            device_id_type=MESH,
        )

    own = pltpu.make_async_copy(
        packed.at[expert, shard], received.at[task, place], own_sem
    )
    for de, ds in order:
        if (de, ds) == (0, 0):
            pl.when(is_own)(own.start)
            pl.when(jnp.logical_not(is_own))(outgoing(de, ds).start)
        else:
            outgoing(de, ds).start()
    for from_task in range(tasks):
        for at in range(group):
            local = jnp.logical_and(is_own, jnp.logical_and(task == from_task, place == at))
            arriving = pltpu.make_async_remote_copy(
                src_ref=packed.at[0, 0],
                dst_ref=received.at[from_task, at],
                send_sem=send_sem.at[0, 0],
                recv_sem=recv_sem.at[from_task, at],
                device_id=(lax.rem(expert + 1, experts), task, shard),
                device_id_type=MESH,
            )
            pl.when(jnp.logical_not(local))(arriving.wait_recv)
    for de, ds in order:
        if (de, ds) == (0, 0):
            pl.when(is_own)(own.wait)
            pl.when(jnp.logical_not(is_own))(outgoing(de, ds).wait_send)
        else:
            outgoing(de, ds).wait_send()


def exchange(packed, sizes):
    experts, tasks, shards = sizes
    group = experts * shards // tasks
    return pl.pallas_call(
        functools.partial(exchange_body, sizes),
        out_shape=jax.ShapeDtypeStruct((tasks, group) + packed.shape[2:], packed.dtype),
        in_specs=[pl.BlockSpec(memory_space=pl.ANY)],
        out_specs=pl.BlockSpec(memory_space=pl.ANY),
        scratch_shapes=[
            pltpu.SemaphoreType.DMA((experts, shards)),
            pltpu.SemaphoreType.DMA((tasks, group)),
            pltpu.SemaphoreType.DMA,
        ],
        compiler_params=pltpu.CompilerParams(has_side_effects=True),
        name="exchange",
    )(packed)


def merge_body(tasks, slots, live, *refs):
    parts, base, merged = refs[:tasks], refs[tasks], refs[tasks + 1]
    at = pl.program_id(0) * pl.num_programs(1) + pl.program_id(1)
    count = pl.num_programs(0) * pl.num_programs(1)
    numerator = PRIOR_WEIGHT * base[...].astype(jnp.float32)
    denominator = jnp.full(base.shape, PRIOR_WEIGHT, jnp.float32)
    for task, part in enumerate(parts):
        kept = live[task * count + at].astype(jnp.float32)
        numerator += part[0, 0, 0, 0].astype(jnp.float32) * kept
        denominator += part[0, 0, 1, 0].astype(jnp.float32) * kept
    merged[...] = (numerator / denominator).astype(jnp.bfloat16)


def merge(slots, live, received, base):
    tasks, group, _, _, _, width = received.shape
    per_block = slots.shape[0] // (tasks * group)

    def part(task):
        return pl.BlockSpec(
            (1, 1, 2, 1, TILE, width),
            lambda g, j, slots, live: (
                task, g, 0, slots[(task * group + g) * per_block + j], 0, 0
            ),
        )

    rows = pl.BlockSpec((TILE, width), lambda g, j, slots, live: (g * per_block + j, 0))
    return pl.pallas_call(
        functools.partial(merge_body, tasks),
        out_shape=jax.ShapeDtypeStruct(base.shape, jnp.bfloat16),
        grid_spec=pltpu.PrefetchScalarGridSpec(
            num_scalar_prefetch=2,
            grid=(group, per_block),
            in_specs=[part(task) for task in range(tasks)] + [rows],
            out_specs=rows,
        ),
        name="merge",
    )(slots, live, *([received] * tasks), base)


def mesh_copy(source, target, send_sem, recv_sem, device):
    return pltpu.make_async_remote_copy(
        src_ref=source, dst_ref=target, send_sem=send_sem, recv_sem=recv_sem,
        device_id=device, device_id_type=MESH,
    )


def fused_body(
    plan, plan_hbm, weights, fisher, base, merged,
    w_buf, f_buf, packed, gathered, sums, direct, far, base_buf, out_buf,
    plans, tables, slots, live,
    in_sem, base_sem, out_sem, p_send, p_recv, table_sem,
    g_send, g_recv, g_own, n_send, n_recv, n_own, s_send, s_recv,
):
    expert, task, shard = (lax.axis_index(a) for a in ("expert", "task", "shard"))
    x, y, half = task % 2, task // 2, shard // 2
    cap = packed[0].shape[2]
    tiles = sums[0].shape[1]
    width = packed[0].shape[-1]
    rows = far[0].shape[3]
    owner = 2 * expert + half
    block = 4 * expert + shard
    is_near = x == half
    columns = [3 - shard, (shard + 2) % 4, shard + 1 - 2 * (shard % 2), shard]

    def load(i):
        lanes = pl.ds(pl.multiple_of(columns[i] * width, width), width)
        return (
            pltpu.make_async_copy(weights.at[:, :, :, lanes], w_buf[i], in_sem.at[i, 0]),
            pltpu.make_async_copy(fisher.at[:, :, :, lanes], f_buf[i], in_sem.at[i, 1]),
        )

    def pack(i):
        for copy in load(i):
            copy.wait()

        def step(n, carry):
            e, k = n // cap, n % cap
            tile = jnp.minimum(plan[0, (e * 8 + block) * cap + k], tiles - 1)
            share = f_buf[i][e, tile]
            packed[i][e, 0, k] = share * w_buf[i][e, tile]
            packed[i][e, 1, k] = share
            return carry

        lax.fori_loop(0, 2 * cap, step, 0)

    def gather(i, de, dx):
        to_expert, to_x = (expert + de) % 2, (x + dx) % 2
        start = pl.multiple_of(DIRECT + rows * to_x, 16)
        part = packed[i].at[to_expert, :, :, pl.ds(start, rows)]
        target = gathered[i].at[task]
        return part, target, mesh_copy(
            part, target, g_send.at[i, de, dx], g_recv.at[i, task], (to_expert, 2 * expert + to_x, shard)
        )

    def straight(i, de, g):
        to_expert = (expert + de) % 2
        part = packed[i].at[to_expert, :, :, pl.ds(DIRECT * g, DIRECT)]
        target = direct[i % 2][g].at[task]
        return part, target, mesh_copy(
            part, target, n_send.at[i, de, g], n_recv.at[i % 2, g, task], (to_expert, owner, columns[i])
        )

    def start(copy, own, sem):
        part, target, remote = copy
        if own is None:
            remote.start()
        else:
            pl.when(own)(pltpu.make_async_copy(part, target, sem).start)
            pl.when(jnp.logical_not(own))(remote.start)

    def reduced(i):
        return mesh_copy(
            sums[i], far[i].at[x], s_send.at[i], s_recv.at[i, x], (expert, 2 * y + half, columns[i])
        )

    def tell(step):
        return mesh_copy(
            plan_hbm, plans.at[task], p_send.at[step], p_recv.at[task], (expert, (task + step) % 4, shard)
        )

    def come(target, sem):
        return mesh_copy(target, target, p_send.at[0], sem, (1 - expert, task, shard))

    for i in range(4):
        for copy in load(i):
            copy.start()
    get_base = pltpu.make_async_copy(base, base_buf, base_sem)
    get_base.start()
    me = (expert * 4 + task) * 4 + shard
    barrier = pltpu.get_barrier_semaphore()

    def greet(n, carry):
        @pl.when(n != me)
        def _():
            pl.semaphore_signal(barrier, inc=1, device_id=(n // 16, (n // 4) % 4, n % 4), device_id_type=MESH)

        return carry

    lax.fori_loop(0, 32, greet, 0)
    pack(0)
    pl.semaphore_wait(barrier, 31)

    own_plan = pltpu.make_async_copy(plan_hbm, plans.at[task], table_sem.at[0])
    own_plan.start()
    for step in range(1, 4):
        tell(step).start()

    gather_own = jnp.logical_and(expert == y, True)
    near_own = jnp.logical_and(expert == y, is_near)

    def send_far(i):
        for de in range(2):
            for dx in (1, 0):
                start(gather(i, de, dx), gather_own if de == 0 and dx == 0 else None, g_own.at[i])
        for de in range(2):
            start(straight(i, de, 0), None, None)

    def send_near(i):
        for g in range(len(direct[0])):
            for de in range(2):
                start(straight(i, de, g), near_own if i == 3 and de == 0 else None, n_own.at[g])

    send_far(0)
    pack(1)
    send_far(1)
    pack(2)
    send_near(2)
    pack(3)
    send_near(3)

    own_plan.wait()
    for source in range(4):
        pl.when(task != source)(come(plans.at[source], p_recv.at[source]).wait_recv)
    fetch = pltpu.make_async_copy(plans, tables, table_sem.at[1])
    fetch.start()
    fetch.wait()
    blocks = [4 * y + shard, 4 * y + 2 * x + 1 - shard % 2, 4 * y + 2 * x + shard % 2]

    def look(n, carry):
        t, tile = n // tiles, n % tiles
        for which, at in enumerate(blocks):
            slot, found = jnp.int32(0), jnp.int32(0)
            for k in range(cap):
                hit = (tables[t, 0, (expert * 8 + at) * cap + k] == tile).astype(jnp.int32)
                slot = jnp.maximum(slot, hit * k)
                found = jnp.maximum(found, hit)
            slots[which, n] = slot
            live[which, n] = found
        return carry

    lax.fori_loop(0, 4 * tiles, look, 0)

    def kept(which, tile):
        return [
            (slots[which, t * tiles + tile], live[which, t * tiles + tile].astype(jnp.float32)) for t in range(4)
        ]

    def added(ref, which, terms):
        return sum(ref[t, which, s].astype(jnp.float32) * k for t, (s, k) in enumerate(terms))

    for i in range(2):
        for source in range(4):
            own = jnp.logical_and(expert == y, task == source)
            part, target, _ = gather(i, 0, 0)
            pl.when(own)(pltpu.make_async_copy(part, target, g_own.at[i]).wait)
            pl.when(jnp.logical_not(own))(come(gathered[i].at[source], g_recv.at[i, source]).wait_recv)

        def total(tile, carry, i=i):
            terms = kept(0, tile)
            for which in range(2):
                sums[i][which, tile] = added(gathered[i], which, terms).astype(jnp.bfloat16)
            return carry

        lax.fori_loop(0, tiles, total, 0)
        reduced(i).start()

    get_base.wait()

    def settle(at, span, numerator, denominator):
        numerator += PRIOR_WEIGHT * base_buf[at, span].astype(jnp.float32)
        out_buf[at, span] = (numerator / (denominator + PRIOR_WEIGHT)).astype(jnp.bfloat16)

    def deliver(k, first):
        place = (shard + 1 + k) % 2
        group = pl.ds(pl.multiple_of(place * tiles, tiles), tiles)

        def arrived(g, own_too):
            for source in range(4):
                arrive = come(direct[k][g].at[source], n_recv.at[k, g, source])
                if own_too:
                    own = jnp.logical_and(expert == y, task == source)
                    part, target, _ = straight(3, 0, g)
                    pl.when(own)(pltpu.make_async_copy(part, target, n_own.at[g]).wait)
                    pl.when(jnp.logical_not(own))(arrive.wait_recv)
                else:
                    arrive.wait_recv()

        def plain(g):
            span = pl.ds(DIRECT * g, DIRECT)

            def one(tile, carry):
                terms = kept(1 + k, tile)
                settle(place * tiles + tile, span, added(direct[k][g], 0, terms), added(direct[k][g], 1, terms))
                return carry

            lax.fori_loop(0, tiles, one, 0)

        def write(g, count):
            span = pl.ds(DIRECT * g, DIRECT * count)
            return pltpu.make_async_copy(
                out_buf.at[group, span], merged.at[group, span], out_sem.at[k, g]
            )

        groups = len(direct[0])

        @pl.when(is_near)
        def _():
            for g in range(groups):
                if first:
                    arrived(g, k == 1)
                    plain(g)
                    write(g, 1).start()
                else:
                    write(g, 1).wait()

        @pl.when(jnp.logical_not(is_near))
        def _():
            if not first:
                write(0, groups).wait()
                return
            arrived(0, False)
            plain(0)
            for source in range(2):
                come(far[k].at[source], s_recv.at[k, source]).wait_recv()

            def one(tile, carry):
                for source in range(2):
                    settle(
                        place * tiles + tile,
                        pl.ds(DIRECT + rows * source, rows),
                        far[k][source, 0, tile].astype(jnp.float32),
                        far[k][source, 1, tile].astype(jnp.float32),
                    )
                return carry

            lax.fori_loop(0, tiles, one, 0)
            write(0, groups).start()

    deliver(0, True)
    deliver(1, True)
    for step in range(1, 4):
        tell(step).wait_send()
    for i in range(2):
        for de in range(2):
            for dx in range(2):
                remote = gather(i, de, dx)[2]
                if de == 0 and dx == 0:
                    pl.when(jnp.logical_not(gather_own))(remote.wait_send)
                else:
                    remote.wait_send()
            straight(i, de, 0)[2].wait_send()
        reduced(i).wait_send()
    for i in (2, 3):
        for g in range(len(direct[0])):
            for de in range(2):
                remote = straight(i, de, g)[2]
                if i == 3 and de == 0:
                    pl.when(jnp.logical_not(near_own))(remote.wait_send)
                else:
                    remote.wait_send()
    deliver(0, False)
    deliver(1, False)


def fused(plan, weights, fisher, base):
    experts, tiles, _, columns = weights.shape
    width = base.shape[-1]
    cap = plan.shape[1] // 2 // 16
    groups = TILE // DIRECT
    rows = (TILE - DIRECT) // 2
    b16 = lambda *shape: pltpu.VMEM(shape, jnp.bfloat16)
    dma = lambda *shape: pltpu.SemaphoreType.DMA(shape)
    anywhere = pl.BlockSpec(memory_space=pl.ANY)
    scratch = [
        [b16(experts, tiles, TILE, width) for _ in range(4)],
        [b16(experts, tiles, TILE, width) for _ in range(4)],
        [b16(experts, 2, cap, TILE, width) for _ in range(4)],
        [b16(4, 2, cap, rows, width) for _ in range(2)],
        [b16(2, tiles, rows, width) for _ in range(2)],
        [[b16(4, 2, cap, DIRECT, width) for _ in range(groups)] for _ in range(2)],
        [b16(2, 2, tiles, rows, width) for _ in range(2)],
        b16(*base.shape),
        b16(*base.shape),
        pltpu.VMEM((4,) + plan.shape, jnp.int32),
        pltpu.SMEM((4,) + plan.shape, jnp.int32),
        pltpu.SMEM((3, 4 * tiles), jnp.int32),
        pltpu.SMEM((3, 4 * tiles), jnp.int32),
        dma(4, 2), pltpu.SemaphoreType.DMA, dma(2, groups), dma(4), dma(4), dma(2),
        dma(2, 2, 2), dma(2, 4), dma(2), dma(4, 2, groups), dma(2, groups, 4), dma(groups), dma(2), dma(2, 2),
    ]
    return pl.pallas_call(
        fused_body,
        out_shape=jax.ShapeDtypeStruct(base.shape, jnp.bfloat16),
        in_specs=[pl.BlockSpec(memory_space=pltpu.SMEM)] + [anywhere] * 4,
        out_specs=anywhere,
        scratch_shapes=scratch,
        compiler_params=pltpu.CompilerParams(
            has_side_effects=True, collective_id=0, vmem_limit_bytes=60 * 1024 * 1024
        ),
        name="fused",
    )(plan, plan, weights, fisher, base)


def local(weights, fisher, base_weights, tile_list, tile_count):
    experts, tasks, shards = (lax.axis_size(a) for a in ("expert", "task", "shard"))
    expert, task, shard = (lax.axis_index(a) for a in ("expert", "task", "shard"))
    per_block = weights.shape[2] // TILE
    cap = tile_list.shape[-1]
    group = experts * shards // tasks
    block = expert * shards + shard
    slot_number = jnp.arange(cap, dtype=jnp.int32)
    marked = jnp.where(slot_number < tile_count[..., None], tile_list, per_block)

    if (experts, tasks, shards, weights.shape[1]) == (2, 4, 4, 2):
        base = base_weights[0]
        plan = jnp.pad(marked.reshape(1, -1), ((0, 0), (0, marked.size)))
        blocks = base.reshape(-1, TILE, base.shape[-1])
        tiled = (weights.shape[1], per_block, TILE, weights.shape[3])
        return fused(plan, weights.reshape(tiled), fisher.reshape(tiled), blocks).reshape(base.shape)[None]

    own_list = lax.dynamic_index_in_dim(tile_list[0], block, 1, keepdims=False)
    own_count = lax.dynamic_index_in_dim(tile_count[0], block, 1, keepdims=False)
    own_live = (slot_number[None, :] < own_count[:, None]).astype(jnp.int32)
    packed = pack(own_list.reshape(-1), own_live.reshape(-1), weights[0], fisher[0], shards)
    plans = lax.all_gather(marked[0], "task")
    plans = lax.dynamic_index_in_dim(plans, expert, 1, keepdims=False)
    part = lax.dynamic_slice_in_dim(plans, task * group, group, 1)
    hits = part[..., None] == jnp.arange(per_block, dtype=jnp.int32)
    slots = jnp.sum(hits * slot_number[:, None], axis=2).astype(jnp.int32).reshape(-1)
    live = jnp.any(hits, axis=2).astype(jnp.int32).reshape(-1)
    received = exchange(packed, (experts, tasks, shards))
    return merge(slots, live, received, base_weights[0])[None]


def solution(mesh):
    in_specs = (
        P("task", None, ("expert", "shard"), None),
        P("task", None, ("expert", "shard"), None),
        P("expert", "task", "shard"),
        P("task", None, None, None),
        P("task", None, None),
    )
    out_specs = P("expert", "task", "shard")
    return jax.shard_map(local, mesh=mesh, in_specs=in_specs, out_specs=out_specs, check_vma=False)
```

time: 184 us -> 140 us (0.76)
  Pallas kernels: 176 us -> 135 us
  local copies, waits for them, and re-layouts: 6.87 us -> 3.74 us
    pallas_call x5 -> x1, Pallas kernels: 176 us -> 135 us  [fused(): pl.pallas_call(fused_body, out_shape=jax.ShapeDtypeStruct(base.shape, jnp...]
    unnamed x4 -> x1, local copies, waits for them, and re-layouts: 0.01 us -> 3.05 us
    dynamic_slice x5 -> x0, local copies, waits for them, and re-layouts: 2.55 us -> none  [the longest x2 1.45 us: lookup(): part = lax.dynamic_slice_in_dim(plans, start, count, 1)]
where the time goes in v1:
time: 140 us
  Pallas kernels  135 us (96%)
  local copies, waits for them, and re-layouts  3.74 us (3%)
    pallas_call x1, Pallas kernels, fused(): pl.pallas_call(fused_body, out_shape=jax.ShapeDtypeStruct(base.shape, jnp...  135 us
    unnamed x1, local copies, waits for them, and re-layouts  3.05 us

profile of v1, /device:TPU:1, one launch (start us, length us, event | category | flops | bytes accessed | tf_op | source)
XLA Modules:
  0.0 140.0 jit_solution(14956403686906863984)
XLA Ops:
  0.0 0.7 fusion
  0.7 0.1 copy.7
  0.8 0.1 reshape.20
  0.9 0.5 pad.4.plan.plan_hbm
  1.4 135.5 %fused.1 = bf16[16,128,512]{2,1,0:T(8,128)(2,1)} custom-call(s32[1,128]{1,0:T(1,128)} %pad.4.plan.plan_hbm, s32[1,128]{1,0:T(1,128)} %pad.4.plan.plan_hbm, bf16[2,8,128,2048]{3,2,1,0:T(8,128)(2,1)} %bitcast.7, bf16[2,8,128,2048]{3,2,1,0:T(8,128)(2,1)} %bitcast.8, bf16[16,128,512]{2,1,0:T(8,128)(2,1)} %bitcast.10), custom_call_target="tpu_custom_call" | custom-call | tf_op jit(solution)/shard_map/fused/pallas_call | solution.py:462
  136.9 3.0 %copy.9 = bf16[1,2048,512]{2,1,0:T(8,128)(2,1)} copy(bf16[1,2048,512]{2,1,0:T(8,128)(2,1)} %bitcast.9) | data formatting | bytes 4194304
